TPU v7x, 32 devices: a whole 2x2x4 slice. The times are simulated.
32 devices in a mesh: dp: 4 (over x, core), expert: 8 (over z, y).
Axes of the slice: x: 2, y: 2, z: 4, core: 2. Of those that a mesh axis runs over, the one named last changes fastest.
Arguments:
- queries: bfloat16 [2, 4, 8, 2048], P(None, 'dp', 'expert'), may hold values from -5 to 5
- cache_keys: bfloat16 [4, 8, 512, 512], P('dp', 'expert'), may hold values from -5 to 5
- cache_values: bfloat16 [4, 8, 512, 512], P('dp', 'expert'), may hold values from -6 to 6
- new_keys: bfloat16 [2, 4, 8, 512], P(None, 'dp', 'expert'), may hold values from -9 to 9
- new_values: bfloat16 [2, 4, 8, 512], P(None, 'dp', 'expert'), may hold values from -6 to 6
- cache_len: int32 [4, 8], P('dp', 'expert'), may hold values from 256 to 510, as said below
- o_proj: bfloat16 [2048, 4096], P(None, 'expert'), may hold values from -0.125 to 0.125
- residual_in: bfloat16 [2, 4, 8, 4096], P(None, 'dp', None, 'expert'), may hold values from -36 to 36
- norm_gain: float32 [4096], P('expert'), may hold values from 0.1 to 1.9
- router: float32 [4096, 8], P('expert'), may hold values from -0.09375 to 0.09375
- expert_gate: bfloat16 [8, 4096, 14336], P('expert', None, 'dp'), may hold values from -0.09375 to 0.09375
- expert_up: bfloat16 [8, 4096, 14336], P('expert', None, 'dp'), may hold values from -0.09375 to 0.09375
- expert_down: bfloat16 [8, 14336, 4096], P('expert', 'dp'), may hold values from -0.046875 to 0.046875
- routes: int32 [2, 4, 8, 2], replicated, may hold values from 0 to 7, all different within a row; in each aligned block of 8 rows (0 to 7, 8 to 15, ..., all dimensions but the last counted through in order) at most 4 rows name the same one
- answers: int32 [2, 4, 8], P(None, 'dp', 'expert'), may hold values from 0 to 127
- stop_mask: int32 [2, 4], P(None, 'dp'), may hold values 0 or 1
Outputs:
- residual_out: bfloat16 [2, 4, 8, 4096], P(None, 'dp', None, 'expert')
- vote_share: float32 [2, 4, 128], P(None, 'dp')
Inputs may be any that keep to these rules, and one draw needn't show every extreme that they name: `cache_len`: some sequence uses exactly 510 cached positions. `routes`: each token names 2 different experts; in each step, the tokens of the 1 prompts of one index of dp (all their samples together) name one expert at most 4 times.
All inputs are finite; a program needn't handle non-finite values. No bound on the sum of `stop_mask` on one device may be relied on, other than what follows from the above.
Results may differ from a plain program's by a relative error of at most 0.0055.
Values may be sent and summed in bfloat16 or wider, within the bound.
No kernel may reach another device: no remote copies, remote signals or barrier semaphores. Data moves between devices by JAX's collectives and lax.ppermute only.
A program may use at most 192 MiB of HBM per device.

v0:
```python
import jax
import jax.numpy as jnp
from jax import lax
from jax.sharding import PartitionSpec as P

D = 4096
E = 8
TOP = 2
HD = 128
QH = 16
KVH = 4
STEPS = 2
ANSWERS = 128
EPSILON = 1e-05


def attend(query, keys, values, fresh_keys, fresh_values, lengths):
    step_count = query.shape[0]
    row_count = query.shape[1]
    cache_size = keys.shape[1]
    group_size = QH // KVH
    score_scale = HD ** (-0.5)
    queried = query.reshape(step_count, row_count, KVH, group_size, HD)
    old_keys = keys.reshape(row_count, cache_size, KVH, HD)
    old_values = values.reshape(row_count, cache_size, KVH, HD)
    young_keys = fresh_keys.reshape(step_count, row_count, KVH, HD)
    young_values = fresh_values.reshape(step_count, row_count, KVH, HD)
    old_scores = (
        jnp.einsum("trkgd,rckd->rkgtc", queried, old_keys, preferred_element_type=jnp.float32)
        * score_scale
    )
    new_scores = (
        jnp.einsum("trkgd,urkd->rkgtu", queried, young_keys, preferred_element_type=jnp.float32)
        * score_scale
    )
    old_valid = jnp.arange(cache_size, dtype=jnp.int32)[None, :] < lengths[:, None]
    old_scores = jnp.where(old_valid[:, None, None, None, :], old_scores, -jnp.inf)
    new_valid = jnp.arange(step_count)[None, :] <= jnp.arange(step_count)[:, None]
    new_scores = jnp.where(new_valid, new_scores, -jnp.inf)
    highest = jnp.maximum(jnp.max(old_scores, -1), jnp.max(new_scores, -1))[..., None]
    old_exp = jnp.exp(old_scores - highest)
    new_exp = jnp.exp(new_scores - highest)
    denominator = jnp.sum(old_exp, -1, keepdims=True) + jnp.sum(new_exp, -1, keepdims=True)
    old_weights = (old_exp / denominator).astype(jnp.bfloat16)
    new_weights = (new_exp / denominator).astype(jnp.bfloat16)
    combined = jnp.einsum(
        "rkgtc,rckd->trkgd", old_weights, old_values, preferred_element_type=jnp.float32
    )
    combined = combined + jnp.einsum(
        "rkgtu,urkd->trkgd", new_weights, young_values, preferred_element_type=jnp.float32
    )
    return combined.reshape(step_count, row_count, QH * HD).astype(jnp.bfloat16)


def slot_tables(picks, capacity):
    block_count = picks.shape[0]
    row_count = picks.shape[1]
    expert_hot = (picks[..., None] == jnp.arange(E, dtype=jnp.int32)).astype(jnp.int32)
    expert_hot = expert_hot.reshape(block_count, row_count * TOP, E)
    earlier = jnp.cumsum(expert_hot, 1) - expert_hot
    place = jnp.sum(earlier * expert_hot, -1).reshape(block_count, row_count, TOP)
    slot_ids = picks * capacity + place
    return (slot_ids[..., None] == jnp.arange(E * capacity, dtype=jnp.int32)).astype(jnp.float32)


def on_device(
    queries,
    cache_keys,
    cache_values,
    new_keys,
    new_values,
    cache_len,
    o_proj,
    residual_in,
    norm_gain,
    router,
    expert_gate,
    expert_up,
    expert_down,
    routes,
    answers,
    stop_mask,
):
    prompt_dev = residual_in.shape[1]
    samples = residual_in.shape[2]
    columns = residual_in.shape[3]
    local_count = queries.shape[2]
    seq_count = prompt_dev * local_count
    cache_size = cache_keys.shape[2]
    spread = lax.axis_size("expert") // E
    capacity = 2 * prompt_dev * samples * TOP // E
    block_rows = prompt_dev * samples
    dp_index = lax.axis_index("dp")
    attended = attend(
        queries.reshape(STEPS, seq_count, QH * HD),
        cache_keys.reshape(seq_count, cache_size, KVH * HD),
        cache_values.reshape(seq_count, cache_size, KVH * HD),
        new_keys.reshape(STEPS, seq_count, KVH * HD),
        new_values.reshape(STEPS, seq_count, KVH * HD),
        cache_len.reshape(seq_count),
    ).reshape(STEPS, prompt_dev, local_count, QH * HD)
    active = (1 - stop_mask).astype(jnp.float32)
    attn_proj = jnp.einsum(
        "tpsq,qc->tpsc",
        lax.all_gather(attended, "expert", axis=2, tiled=True),
        o_proj,
        preferred_element_type=jnp.float32,
    )
    mixed_rows = residual_in.astype(jnp.float32) + attn_proj
    squares = jnp.sum(mixed_rows * mixed_rows, -1)
    scaled = mixed_rows * norm_gain
    squares_all = lax.psum(squares, "expert")
    inv_rms = lax.rsqrt(squares_all / D + EPSILON)[..., None]
    normed_f = scaled * inv_rms
    partial_logits = jnp.einsum("tpsc,ce->tpse", normed_f, router, precision=lax.Precision.HIGHEST)
    logits = lax.psum(partial_logits, "expert")
    normed = normed_f.astype(jnp.bfloat16)
    own_picks = lax.dynamic_slice_in_dim(routes, dp_index * prompt_dev, prompt_dev, 1)
    expert_hot = (own_picks[..., None] == jnp.arange(E, dtype=jnp.int32)).astype(jnp.float32)
    chosen = jnp.sum(expert_hot * logits[:, :, :, None, :], -1)
    gate_weights = jax.nn.sigmoid(chosen - chosen[..., ::-1]).reshape(STEPS, block_rows, TOP)
    own_table = slot_tables(own_picks.reshape(STEPS, block_rows, TOP), capacity)
    senders = jnp.sum(own_table, 2).astype(jnp.bfloat16)
    outgoing = jnp.einsum(
        "trs,trx->tsx",
        senders,
        normed.reshape(STEPS, block_rows, columns),
        preferred_element_type=jnp.float32,
    ).astype(jnp.bfloat16)
    outgoing = jnp.transpose(outgoing.reshape(STEPS, E, capacity, columns), (1, 0, 2, 3)).reshape(
        E, 1, STEPS * capacity, columns
    )
    outgoing = jnp.broadcast_to(outgoing, (E, spread, STEPS * capacity, columns)).reshape(
        E * spread, STEPS * capacity, columns
    )
    tokens = lax.all_gather(
        lax.all_to_all(outgoing, "expert", split_axis=0, concat_axis=2, tiled=True),
        "dp",
        axis=0,
        tiled=True,
    )
    gate_part = jnp.einsum(
        "...d,df->...f", tokens, expert_gate[0], preferred_element_type=jnp.float32
    )
    up_part = jnp.einsum("...d,df->...f", tokens, expert_up[0], preferred_element_type=jnp.float32)
    hidden = (jax.nn.silu(gate_part) * up_part).astype(jnp.bfloat16)
    partial_out = lax.psum_scatter(
        jnp.einsum("...f,fd->...d", hidden, expert_down[0], preferred_element_type=jnp.float32),
        "dp",
        scatter_dimension=0,
        tiled=True,
    )
    returned = lax.all_to_all(partial_out, "expert", split_axis=2, concat_axis=0, tiled=True)
    slot_out = jnp.sum(returned.reshape(E, spread, STEPS, capacity, columns), 1)
    slot_out = jnp.transpose(slot_out, (1, 0, 2, 3)).reshape(STEPS, E * capacity, columns)
    combine = jnp.einsum("trk,trks->trs", gate_weights, own_table)
    moe = jnp.einsum("trs,tsx->trx", combine, slot_out, precision=lax.Precision.HIGHEST).reshape(
        STEPS, prompt_dev, samples, columns
    )
    updated = residual_in.astype(jnp.float32) + active[:, :, None, None] * (attn_proj + moe)
    hits = jnp.sum(
        (answers[..., None] == jnp.arange(ANSWERS, dtype=jnp.int32)).astype(jnp.float32), 2
    )
    votes = active[:, :, None] * hits
    tallied = lax.psum(votes, "expert")
    running = jnp.cumsum(tallied, 0)
    shares = running / jnp.maximum(jnp.sum(running, -1, keepdims=True), 1.0)
    return (updated.astype(jnp.bfloat16), shares)


def solution(mesh):
    placed = (
        P(None, "dp", "expert", None),
        P("dp", "expert", None, None),
        P("dp", "expert", None, None),
        P(None, "dp", "expert", None),
        P(None, "dp", "expert", None),
        P("dp", "expert"),
        P(None, "expert"),
        P(None, "dp", None, "expert"),
        P("expert"),
        P("expert", None),
        P("expert", None, "dp"),
        P("expert", None, "dp"),
        P("expert", "dp", None),
        P(),
        P(None, "dp", "expert"),
        P(None, "dp"),
    )
    return jax.shard_map(
        on_device,
        mesh=mesh,
        in_specs=placed,
        out_specs=(P(None, "dp", None, "expert"), P(None, "dp", None)),
        check_vma=False,
    )
```

profile of v0, /device:TPU:0, one launch (start us, length us, event | category | flops | bytes accessed | tf_op | source)
XLA Modules:
  0.0 199.6 jit_solution(14043567168421434307)
XLA Ops:
  7.2 0.9 reshape.296
  8.1 1.2 reshape.295
  9.9 0.9 convolution_multiply_fusion.1
  11.6 1.2 reshape.299
  13.0 0.9 fusion.25
  13.9 32.4 %all_gather.6 = bf16[2,1,8,2048]{3,0,1,2:T(2,128)(2,1)S(1)} all-gather(bf16[2,1,1,2048]{3,0,1,2:T(2,128)(2,1)S(1)} %bitcast.171), channel_id=1, replica_groups=mesh['dp'=4,'expert'=8] {'expert'}, dimensions={2}, use_global_device_ids=true | all-gather | bytes 73728 | tf_op jit(solution)/shard_map/all_gather | solution.py:105
  46.3 1.2 multiply_reduce_fusion
  47.4 21.3 %psum.21 = f32[2,1,8]{2,0,1:T(2,128)S(1)} all-reduce(f32[2,1,8]{2,0,1:T(2,128)S(1)} %bitcast.173), channel_id=1, replica_groups=mesh['dp'=4,'expert'=8] {'expert'}, use_global_device_ids=true, to_apply=%region_5.6 | all-reduce | flops 16 | bytes 128 | tf_op jit(solution)/shard_map/psum | solution.py:112
  70.9 0.9 convolution_convert_fusion
  72.5 3.3 %all-to-all-start = ((bf16[8,8,512]{2,1,0:T(8,128)(2,1)}), bf16[8,8,512]{2,1,0:T(8,128)(2,1)S(1)}, u32[]{:S(2)}, u32[]{:S(2)}) async-start(bf16[8,8,512]{2,1,0:T(8,128)(2,1)} %copy.113), calls=%async_computation | async-start | bytes 131072 | tf_op jit(solution)/shard_map/all_to_all | solution.py:137
  75.9 1.0 fusion.38
  78.3 4.4 %all-to-all-done = bf16[8,8,512]{2,1,0:T(8,128)(2,1)S(1)} async-done(((bf16[8,8,512]{2,1,0:T(8,128)(2,1)}), bf16[8,8,512]{2,1,0:T(8,128)(2,1)S(1)}, u32[]{:S(2)}, u32[]{:S(2)}) %all-to-all-start) | async-done | bytes 65568 | tf_op jit(solution)/shard_map/all_to_all | solution.py:137
  82.7 5.8 %all_gather.7 = bf16[4,8,4096]{2,1,0:T(8,128)(2,1)S(1)} all-gather(bf16[1,8,4096]{2,1,0:T(8,128)(2,1)S(1)} %bitcast.169), channel_id=1, replica_groups=mesh['dp'=4,'expert'=8] {'dp'}, dimensions={0}, use_global_device_ids=true | all-gather | bytes 327680 | tf_op jit(solution)/shard_map/all_gather | solution.py:136
  88.5 11.8 %fusion.4 = f32[4,8,3584]{2,1,0:T(8,128)S(1)} fusion(bf16[4,8,4096]{2,1,0:T(8,128)(2,1)S(1)} %all_gather.7, bf16[1,4096,3584]{2,1,0:T(8,128)(2,1)} %param.26), kind=kOutput, calls=%fused_computation.4 | convolution fusion | flops 939524096 | bytes 30081024 | tf_op jit(solution)/shard_map/...d,df->...f/dot_general | solution.py:142
  100.3 22.4 %fusion = f32[4,8,4096]{2,1,0:T(8,128)} fusion(bf16[1,3584,4096]{2,1,0:T(8,128)(2,1)} %param.28, bf16[4,8,4096]{2,1,0:T(8,128)(2,1)S(1)} %all_gather.7, bf16[1,4096,3584]{2,1,0:T(8,128)(2,1)} %param.27, f32[4,8,3584]{2,1,0:T(8,128)S(1)} %fusion.4), kind=kOutput, calls=%fused_computation | convolution fusion | flops 1879736320 | bytes 59965440 | tf_op jit(solution)/shard_map/...f,fd->...d/dot_general | solution.py:148
  123.4 18.6 %all-reduce = (f32[2,8,8]{2,1,0:T(8,128)S(1)}, f32[2,1,128]{2,1,0:T(1,128)S(1)}) all-reduce(f32[2,8,8]{2,1,0:T(8,128)S(1)} %fusion.38, f32[2,1,128]{2,1,0:T(1,128)S(1)} %compare_select_fusion), channel_id=1, replica_groups=mesh['dp'=4,'expert'=8] {'expert'}, use_global_device_ids=true, to_apply=%region_6.7 | all-reduce | flops 384 | bytes 3072 | tf_op jit(solution)/shard_map/psum | solution.py:116
  142.4 4.8 %copy.114 = f32[1,8,4096]{1,0,2:T(1,128)} copy(f32[1,8,4096]{2,1,0:T(8,128)} %reduce-scatter.2.cloned.1.call-done) | data formatting | bytes 262144 | tf_op jit(solution)/shard_map/reduce_scatter | solution.py:147
  147.7 20.4 %reduce.7 = f32[4096,8]{1,0:T(8,128)} reduce(f32[4096,1,8]{2,1,0:T(1,128)} %bitcast.164, f32[]{:T(128)} %broadcast.178), dimensions={1}, to_apply=%bitcast.149.reduce_sub_computation | reduce | bytes 262148
  168.0 3.3 %reshape.320 = f32[8,1,4096]{2,1,0:T(1,128)} reshape(f32[4096,8]{1,0:T(8,128)} %reduce.7) | data formatting | bytes 262144
  171.3 5.1 %all-to-all-start.1 = ((f32[8,1,4096]{2,1,0:T(1,128)}), f32[8,1,4096]{2,1,0:T(1,128)S(1)}, u32[]{:S(2)}, u32[]{:S(2)}) async-start(f32[8,1,4096]{2,1,0:T(1,128)} %reshape.320), calls=%async_computation.2 | async-start | bytes 262144 | tf_op jit(solution)/shard_map/all_to_all | solution.py:153
  177.4 6.5 %all-to-all-done.1 = f32[8,1,4096]{2,1,0:T(1,128)S(1)} async-done(((f32[8,1,4096]{2,1,0:T(1,128)}), f32[8,1,4096]{2,1,0:T(1,128)S(1)}, u32[]{:S(2)}, u32[]{:S(2)}) %all-to-all-start.1) | async-done | bytes 131104 | tf_op jit(solution)/shard_map/all_to_all | solution.py:153
  183.8 1.0 reduce.8
  184.8 4.9 %reshape.321 = f32[4096,1,8]{2,1,0:T(1,128)} reshape(f32[8,4096]{1,0:T(8,128)S(1)} %reduce.8) | data formatting | bytes 262144
  189.6 2.2 %copy.131 = f32[1,8,8,512]{3,2,1,0:T(8,128)S(1)} copy(f32[1,8,8,512]{1,3,2,0:T(8,128)} %bitcast.165) | data formatting | bytes 262144 | tf_op jit(solution)/shard_map/all_to_all | solution.py:153
  (50 shorter events, 8.8 us)
Async XLA Ops:
  7.2 39.1 %copy-start = (bf16[2048,512]{1,0:T(8,128)(2,1)S(1)}, bf16[2048,512]{1,0:T(8,128)(2,1)}, u32[]{:S(2)}) copy-start(bf16[2048,512]{1,0:T(8,128)(2,1)} %param.22) | copy-start | bytes 6291460
  72.5 10.2 %all-to-all-start = ((bf16[8,8,512]{2,1,0:T(8,128)(2,1)}), bf16[8,8,512]{2,1,0:T(8,128)(2,1)S(1)}, u32[]{:S(2)}, u32[]{:S(2)}) async-start(bf16[8,8,512]{2,1,0:T(8,128)(2,1)} %copy.113), calls=%async_computation | async-start | bytes 131072 | tf_op jit(solution)/shard_map/all_to_all | solution.py:137
  75.9 66.5 %reduce-scatter.2.cloned.1.call-start = ((), (), s32[]{:S(2)}) async-start(), calls=%async_computation.3 | async-start | bytes 655360 | tf_op jit(solution)/shard_map/reduce_scatter | solution.py:147
  100.3 91.7 %copy-start.1 = (bf16[2,1,8,512]{3,2,1,0:T(8,128)(2,1)S(1)}, bf16[2,1,8,512]{3,2,1,0:T(8,128)(2,1)}, u32[]{:S(2)}) copy-start(bf16[2,1,8,512]{3,2,1,0:T(8,128)(2,1)} %param.23) | copy-start | bytes 49156
  171.3 12.5 %all-to-all-start.1 = ((f32[8,1,4096]{2,1,0:T(1,128)}), f32[8,1,4096]{2,1,0:T(1,128)S(1)}, u32[]{:S(2)}, u32[]{:S(2)}) async-start(f32[8,1,4096]{2,1,0:T(1,128)} %reshape.320), calls=%async_computation.2 | async-start | bytes 262144 | tf_op jit(solution)/shard_map/all_to_all | solution.py:153
Sparse Core Ops, SparseCore 0:
  122.9 19.1 reduce-scatter.1
where the time goes:
time: 201 us; the launch traced here: 200 us
  blocking collectives  78 us (39%)
  matrix products  40.6 us (20%)
  other arithmetic  25.3 us (13%)
  local copies, waits for them, and re-layouts  21.5 us (11%)
  between operations  14.8 us (7%)
  waiting for transfers between devices  10.9 us (5%)
  starting transfers between devices  8.52 us (4%)
    all_gather x1, blocking collectives, on_device(): lax.all_gather(attended, 'expert', axis=2, tiled=True)  32.4 us
    dot_general x1, matrix products, on_device(): jnp.einsum('...f,fd->...d', hidden, expert_down[0], preferred_element_typ...  22.4 us
    psum x1, blocking collectives, on_device(): squares_all = lax.psum(squares, 'expert')  21.3 us
    unnamed x1, other arithmetic  20.4 us
    psum x1, blocking collectives, on_device(): logits = lax.psum(partial_logits, 'expert')  18.6 us
    dot_general x1, matrix products, on_device(): jnp.einsum('...d,df->...f', tokens, expert_gate[0], preferred_element_typ...  11.8 us
    unnamed x7, local copies, waits for them, and re-layouts  8.7 us
    all_to_all x1, waiting for transfers between devices, on_device(): lax.all_to_all(partial_out, 'expert', split_axis=2, concat_axis=0, tiled=...  6.46 us
  transfers between devices with their start and end apart: 3, of which 2 were waited for; matrix products, arithmetic and copies ran while one was open for 2% of the time, Pallas kernels for 0%

commit v1 on v0

--- a/solution.py
+++ b/solution.py
@@ -150,7 +150,12 @@
         scatter_dimension=0,
         tiled=True,
     )
-    returned = lax.all_to_all(partial_out, "expert", split_axis=2, concat_axis=0, tiled=True)
+    returned = jnp.concatenate(
+        lax.all_to_all(
+            jnp.stack(jnp.split(partial_out, lax.axis_size("expert"), axis=2)), "expert", 0, 0
+        ),
+        axis=0,
+    )
     slot_out = jnp.sum(returned.reshape(E, spread, STEPS, capacity, columns), 1)
     slot_out = jnp.transpose(slot_out, (1, 0, 2, 3)).reshape(STEPS, E * capacity, columns)
     combine = jnp.einsum("trk,trks->trs", gate_weights, own_table)

time: 201 us -> 175 us (0.87)
  other arithmetic: 25.3 us -> 3.96 us
  local copies, waits for them, and re-layouts: 21.5 us -> 16.4 us
    unnamed x1 -> x0, other arithmetic: 20.4 us -> none
    reduce_scatter x1 -> x0, local copies, waits for them, and re-layouts: 4.77 us -> none  [on_device(): lax.psum_scatter(jnp.einsum('...f,fd->...d', hidden, expert_down[0], pref...]
    all_to_all x1 -> x0, local copies, waits for them, and re-layouts: 2.17 us -> none  [on_device(): lax.all_to_all(partial_out, 'expert', split_axis=2, concat_axis=0, tiled=...]
    another operation x4 -> x5, local copies, waits for them, and re-layouts: 3.21 us -> 4.53 us
    unnamed x7 -> x11, local copies, waits for them, and re-layouts: 8.7 us -> 9.23 us
where the time goes in v1:
time: 175 us; the launch traced here: 173 us
  blocking collectives  77.8 us (44%)
  matrix products  40.6 us (23%)
  local copies, waits for them, and re-layouts  16.4 us (9%)
  between operations  14.8 us (8%)
  waiting for transfers between devices  10.9 us (6%)
  starting transfers between devices  8.76 us (5%)
  other arithmetic  3.96 us (2%)
    all_gather x1, blocking collectives, on_device(): lax.all_gather(attended, 'expert', axis=2, tiled=True)  32.4 us
    dot_general x1, matrix products, on_device(): jnp.einsum('...f,fd->...d', hidden, expert_down[0], preferred_element_typ...  22.4 us
    psum x1, blocking collectives, on_device(): squares_all = lax.psum(squares, 'expert')  21.3 us
    psum x1, blocking collectives, on_device(): logits = lax.psum(partial_logits, 'expert')  18.4 us
    dot_general x1, matrix products, on_device(): jnp.einsum('...d,df->...f', tokens, expert_gate[0], preferred_element_typ...  11.8 us
    unnamed x11, local copies, waits for them, and re-layouts  9.23 us
    all_to_all x1, waiting for transfers between devices, on_device(): lax.all_to_all(jnp.stack(jnp.split(partial_out, lax.axis_size('expert'),...  6.46 us
    all_gather x1, blocking collectives, on_device(): lax.all_gather(lax.all_to_all(outgoing, 'expert', split_axis=0, concat_ax...  5.76 us
  transfers between devices with their start and end apart: 3, of which 2 were waited for; matrix products, arithmetic and copies ran while one was open for 2% of the time, Pallas kernels for 0%

profile of v1, /device:TPU:0, one launch (start us, length us, event | category | flops | bytes accessed | tf_op | source)
XLA Modules:
  0.0 173.2 jit_solution(6188954072346993678)
XLA Ops:
  8.1 1.2 reshape.293
  11.6 1.2 reshape.297
  13.0 0.9 fusion.25
  13.9 32.4 %all_gather.6 = bf16[2,1,8,2048]{3,0,1,2:T(2,128)(2,1)S(1)} all-gather(bf16[2,1,1,2048]{3,0,1,2:T(2,128)(2,1)S(1)} %bitcast.196), channel_id=1, replica_groups=mesh['dp'=4,'expert'=8] {'expert'}, dimensions={2}, use_global_device_ids=true | all-gather | bytes 73728 | tf_op jit(solution)/shard_map/all_gather | solution.py:105
  46.3 1.2 multiply_reduce_fusion
  47.4 21.3 %psum.21 = f32[2,1,8]{2,0,1:T(2,128)S(1)} all-reduce(f32[2,1,8]{2,0,1:T(2,128)S(1)} %bitcast.198), channel_id=1, replica_groups=mesh['dp'=4,'expert'=8] {'expert'}, use_global_device_ids=true, to_apply=%region_5.6 | all-reduce | flops 16 | bytes 128 | tf_op jit(solution)/shard_map/psum | solution.py:112
  70.9 0.9 convolution_convert_fusion
  72.5 3.3 %all-to-all-start = ((bf16[8,8,512]{2,1,0:T(8,128)(2,1)}), bf16[8,8,512]{2,1,0:T(8,128)(2,1)S(1)}, u32[]{:S(2)}, u32[]{:S(2)}) async-start(bf16[8,8,512]{2,1,0:T(8,128)(2,1)} %copy.90), calls=%async_computation | async-start | bytes 131072 | tf_op jit(solution)/shard_map/all_to_all | solution.py:137
  75.9 1.0 fusion.38
  78.3 4.4 %all-to-all-done = bf16[8,8,512]{2,1,0:T(8,128)(2,1)S(1)} async-done(((bf16[8,8,512]{2,1,0:T(8,128)(2,1)}), bf16[8,8,512]{2,1,0:T(8,128)(2,1)S(1)}, u32[]{:S(2)}, u32[]{:S(2)}) %all-to-all-start) | async-done | bytes 65568 | tf_op jit(solution)/shard_map/all_to_all | solution.py:137
  82.7 5.8 %all_gather.7 = bf16[4,8,4096]{2,1,0:T(8,128)(2,1)S(1)} all-gather(bf16[1,8,4096]{2,1,0:T(8,128)(2,1)S(1)} %bitcast.194), channel_id=1, replica_groups=mesh['dp'=4,'expert'=8] {'dp'}, dimensions={0}, use_global_device_ids=true | all-gather | bytes 327680 | tf_op jit(solution)/shard_map/all_gather | solution.py:136
  88.5 11.8 %fusion.4 = f32[4,8,3584]{2,1,0:T(8,128)S(1)} fusion(bf16[4,8,4096]{2,1,0:T(8,128)(2,1)S(1)} %all_gather.7, bf16[1,4096,3584]{2,1,0:T(8,128)(2,1)} %param.26), kind=kOutput, calls=%fused_computation.4 | convolution fusion | flops 939524096 | bytes 30081024 | tf_op jit(solution)/shard_map/...d,df->...f/dot_general | solution.py:142
  100.3 22.4 %fusion = f32[4,8,4096]{2,1,0:T(8,128)} fusion(bf16[1,3584,4096]{2,1,0:T(8,128)(2,1)} %param.28, bf16[4,8,4096]{2,1,0:T(8,128)(2,1)S(1)} %all_gather.7, bf16[1,4096,3584]{2,1,0:T(8,128)(2,1)} %param.27, f32[4,8,3584]{2,1,0:T(8,128)S(1)} %fusion.4), kind=kOutput, calls=%fused_computation | convolution fusion | flops 1879736320 | bytes 59965440 | tf_op jit(solution)/shard_map/...f,fd->...d/dot_general | solution.py:148
  123.4 18.4 %all-reduce = (f32[2,8,8]{2,1,0:T(8,128)S(1)}, f32[2,1,128]{2,1,0:T(1,128)S(1)}) all-reduce(f32[2,8,8]{2,1,0:T(8,128)S(1)} %fusion.38, f32[2,1,128]{2,1,0:T(1,128)S(1)} %compare_select_fusion), channel_id=1, replica_groups=mesh['dp'=4,'expert'=8] {'expert'}, use_global_device_ids=true, to_apply=%region_6.7 | all-reduce | flops 384 | bytes 3072 | tf_op jit(solution)/shard_map/psum | solution.py:116
  142.2 1.3 constant_dynamic-update-slice_fusion.7
  143.5 1.3 constant_dynamic-update-slice_fusion.6
  144.8 1.3 constant_dynamic-update-slice_fusion.5
  146.2 1.3 constant_dynamic-update-slice_fusion.4
  147.5 1.3 constant_dynamic-update-slice_fusion.3
  148.8 1.3 constant_dynamic-update-slice_fusion.2
  150.1 1.3 constant_dynamic-update-slice_fusion.1
  151.4 1.3 constant_dynamic-update-slice_fusion
  152.8 5.4 %all-to-all-start.1 = ((f32[8,1,8,512]{3,2,1,0:T(8,128)}), f32[8,1,8,512]{3,2,1,0:T(8,128)S(1)}, u32[]{:S(2)}, u32[]{:S(2)}) async-start(f32[8,1,8,512]{3,2,1,0:T(8,128)} %constant_dynamic-update-slice_fusion), calls=%async_computation.2 | async-start | bytes 262144 | tf_op jit(solution)/shard_map/all_to_all | solution.py:154
  159.0 6.5 %all-to-all-done.1 = f32[8,1,8,512]{3,2,1,0:T(8,128)S(1)} async-done(((f32[8,1,8,512]{3,2,1,0:T(8,128)}), f32[8,1,8,512]{3,2,1,0:T(8,128)S(1)}, u32[]{:S(2)}, u32[]{:S(2)}) %all-to-all-start.1) | async-done | bytes 131104 | tf_op jit(solution)/shard_map/all_to_all | solution.py:154
  (52 shorter events, 9.9 us)
Async XLA Ops:
  7.2 39.1 %copy-start = (bf16[2048,512]{1,0:T(8,128)(2,1)S(1)}, bf16[2048,512]{1,0:T(8,128)(2,1)}, u32[]{:S(2)}) copy-start(bf16[2048,512]{1,0:T(8,128)(2,1)} %param.22) | copy-start | bytes 6291460
  72.5 10.2 %all-to-all-start = ((bf16[8,8,512]{2,1,0:T(8,128)(2,1)}), bf16[8,8,512]{2,1,0:T(8,128)(2,1)S(1)}, u32[]{:S(2)}, u32[]{:S(2)}) async-start(bf16[8,8,512]{2,1,0:T(8,128)(2,1)} %copy.90), calls=%async_computation | async-start | bytes 131072 | tf_op jit(solution)/shard_map/all_to_all | solution.py:137
  75.9 66.3 %reduce-scatter.2.cloned.1.call-start = ((), (), s32[]{:S(2)}) async-start(), calls=%async_computation.3 | async-start | bytes 655360 | tf_op jit(solution)/shard_map/reduce_scatter | solution.py:147
  100.3 65.3 %copy-start.1 = (bf16[2,1,8,512]{3,2,1,0:T(8,128)(2,1)S(1)}, bf16[2,1,8,512]{3,2,1,0:T(8,128)(2,1)}, u32[]{:S(2)}) copy-start(bf16[2,1,8,512]{3,2,1,0:T(8,128)(2,1)} %param.23) | copy-start | bytes 49156
  152.8 12.7 %all-to-all-start.1 = ((f32[8,1,8,512]{3,2,1,0:T(8,128)}), f32[8,1,8,512]{3,2,1,0:T(8,128)S(1)}, u32[]{:S(2)}, u32[]{:S(2)}) async-start(f32[8,1,8,512]{3,2,1,0:T(8,128)} %constant_dynamic-update-slice_fusion), calls=%async_computation.2 | async-start | bytes 262144 | tf_op jit(solution)/shard_map/all_to_all | solution.py:154
Sparse Core Ops, SparseCore 0:
  122.9 19.0 reduce-scatter.1
